TPU v7x, 32 devices: a whole 2x2x4 slice. The times are simulated.
32 devices in a mesh: gx: 4 (over x, core), gy: 8 (over z, y).
Axes of the slice: x: 2, y: 2, z: 4, core: 2. Of those that a mesh axis runs over, the one named last changes fastest.
Arguments:
- populations: float32 [19, 32, 64, 128], P(None, 'gx', 'gy'), may hold values from 0 to 1, as said below
- cell_kind: int32 [32, 64, 128], P('gx', 'gy'), may hold values from 0 to 3, as said below
- outlet_region: int32 [32, 64], P('gx', 'gy'), may hold values from 0 to 63, as said below
Outputs:
- final_populations: float32 [19, 32, 64, 128], P(None, 'gx', 'gy')
- outlet_means: float32 [2, 64], replicated
Inputs may be any that keep to these rules, and one draw needn't show every extreme that they name: `populations`: positive. `cell_kind`: the plane z = 0 is all inlet (2), the plane z = 127 all outlet (3); all other cells are fluid (0) or wall (1). `outlet_region`: every region names at least one column; ids are constant on aligned tiles of 4 x 4 columns.
All inputs are finite; a program needn't handle non-finite values.
Results may differ from a plain program's by a relative error of at most 0.0001.
Values sent between devices are 32-bit elements; how exact they have to be, the bound alone decides.
A program may use at most 64 MiB of HBM per device.

v0:
```python
import jax
import jax.numpy as jnp
from jax import lax
from jax.sharding import PartitionSpec as P

REGIONS = 64
STEPS = 2


VELOCITIES = (
    (0, 0, 0),
    (1, 0, 0),
    (-1, 0, 0),
    (0, 1, 0),
    (0, -1, 0),
    (0, 0, 1),
    (0, 0, -1),
    (1, 1, 0),
    (-1, -1, 0),
    (1, -1, 0),
    (-1, 1, 0),
    (1, 0, 1),
    (-1, 0, -1),
    (1, 0, -1),
    (-1, 0, 1),
    (0, 1, 1),
    (0, -1, -1),
    (0, 1, -1),
    (0, -1, 1),
)
WEIGHTS = (1.0 / 3.0,) + (1.0 / 18.0,) * 6 + (1.0 / 36.0,) * 12
OPPOSITE = (0, 2, 1, 4, 3, 6, 5, 8, 7, 10, 9, 12, 11, 14, 13, 16, 15, 18, 17)
RELAX_TIME = 0.8
INLET_SPEED = 0.05
RISING_X = (1, 7, 9, 11, 13)
FALLING_X = (2, 8, 10, 12, 14)
RISING_Y = (3, 7, 10, 15, 17)
FALLING_Y = (4, 8, 9, 16, 18)


def from_behind(block, axis, distance):
    devices = range(lax.axis_size(axis))
    route = [(i - distance, i) for i in devices if i - distance in devices]
    return lax.ppermute(block, axis, route)


def from_behind_2(value, axis, steps):
    count = lax.axis_size(axis)
    pairs = [(source, (source + steps) % count) for source in range(count)]
    return lax.ppermute(value, axis, pairs)


def momentum(current, direction):
    total = jnp.zeros_like(current[0])
    for number in range(19):
        factor = VELOCITIES[number][direction]
        if factor != 0:
            total = total + factor * current[number]
    return total


def equilibrium(density, vel_x, vel_y, vel_z):
    speed_sq = vel_x * vel_x + vel_y * vel_y + vel_z * vel_z
    result = []
    for number in range(19):
        comp_x, comp_y, comp_z = VELOCITIES[number]
        projected = comp_x * vel_x + comp_y * vel_y + comp_z * vel_z
        result.append(
            WEIGHTS[number]
            * density
            * (1.0 + 3.0 * projected + 4.5 * projected * projected - 1.5 * speed_sq)
        )
    return jnp.stack(result)


def collide(current, kinds, col_mean):
    density = jnp.sum(current, axis=0)
    vel_x = momentum(current, 0) / density
    vel_y = momentum(current, 1) / density
    vel_z = momentum(current, 2) / density
    relaxed = current - (current - equilibrium(density, vel_x, vel_y, vel_z)) / RELAX_TIME
    bounced = jnp.stack([current[OPPOSITE[number]] for number in range(19)])
    unity = jnp.ones_like(density)
    still = jnp.zeros_like(density)
    inlet = equilibrium(unity, still, still, INLET_SPEED * unity)
    outlet = equilibrium(col_mean * unity, vel_x, vel_y, vel_z)
    post = jnp.where(kinds == 1, bounced, relaxed)
    post = jnp.where(kinds == 2, inlet, post)
    post = jnp.where(kinds == 3, outlet, post)
    return post


def stream(padded, rows_x, rows_y):
    moved = []
    for number in range(19):
        comp_x, comp_y, comp_z = VELOCITIES[number]
        plane = padded[
            number, 1 - comp_x : 1 - comp_x + rows_x, 1 - comp_y : 1 - comp_y + rows_y, :
        ]
        moved.append(jnp.roll(plane, comp_z, axis=2))
    return jnp.stack(moved)


def outlet_mean(current, kinds, onehot):
    density = jnp.sum(current, axis=0)
    is_outlet = kinds == 3
    column = jnp.sum(jnp.where(is_outlet, density, 0.0), axis=2).reshape(-1)
    col_count = jnp.sum(is_outlet.astype(jnp.float32), axis=2).reshape(-1)
    local_sums = jnp.dot(onehot, column, precision=lax.Precision.HIGHEST)
    local_counts = jnp.dot(onehot, col_count, precision=lax.Precision.HIGHEST)
    totals, counts = lax.psum((local_sums, local_counts), ("gx", "gy"))
    return totals / counts


def widen_first(post, from_lower, from_upper):
    blank = jnp.zeros_like(post[0, :1])
    planes = []
    for number in range(19):
        lower = from_lower[RISING_X.index(number)][None] if number in RISING_X else blank
        upper = from_upper[FALLING_X.index(number)][None] if number in FALLING_X else blank
        planes.append(jnp.concatenate([lower, post[number], upper], axis=0))
    return planes


def widen_second(planes, from_lower, from_upper):
    blank = jnp.zeros_like(planes[0][:, :1])
    padded = []
    for number in range(19):
        lower = from_lower[RISING_Y.index(number)][:, None] if number in RISING_Y else blank
        upper = from_upper[FALLING_Y.index(number)][:, None] if number in FALLING_Y else blank
        padded.append(jnp.concatenate([lower, planes[number], upper], axis=1))
    return jnp.stack(padded)


def body(populations, cell_kind, outlet_region):
    cells_x = populations.shape[1]
    cells_y = populations.shape[2]
    labels = jnp.arange(REGIONS, dtype=jnp.int32)
    onehot = (outlet_region.reshape(-1)[None, :] == labels[:, None]).astype(jnp.float32)
    current = populations
    means = []
    for timestep in range(STEPS):
        region_mean = outlet_mean(current, cell_kind, onehot)
        means.append(region_mean)
        col_mean = jnp.dot(region_mean, onehot, precision=lax.Precision.HIGHEST).reshape(
            cells_x, cells_y
        )[:, :, None]
        post = collide(current, cell_kind, col_mean)
        lower_x = from_behind(jnp.stack([post[number, -1] for number in RISING_X]), "gx", 1)
        upper_x = from_behind(jnp.stack([post[number, 0] for number in FALLING_X]), "gx", -1)
        planes = widen_first(post, lower_x, upper_x)
        lower_y = from_behind_2(jnp.stack([planes[number][:, -1] for number in RISING_Y]), "gy", 1)
        upper_y = from_behind_2(jnp.stack([planes[number][:, 0] for number in FALLING_Y]), "gy", -1)
        padded = widen_second(planes, lower_y, upper_y)
        current = stream(padded, cells_x, cells_y)
    return (current, jnp.stack(means))


def solution(mesh):
    in_specs = (P(None, "gx", "gy", None), P("gx", "gy", None), P("gx", "gy"))
    out_specs = (P(None, "gx", "gy", None), P())
    return jax.shard_map(body, mesh=mesh, in_specs=in_specs, out_specs=out_specs, check_vma=False)
```

profile of v0, /device:TPU:1, one launch (start us, length us, event | category | flops | bytes accessed | tf_op | source)
XLA Modules:
  0.0 127.7 jit_solution(15017054482665278097)
XLA Ops:
  0.7 0.8 constant_dynamic-update-slice_fusion.47
  1.5 1.1 reduce_sum.854
  2.6 0.1 constant_dynamic-update-slice_fusion.66
  2.7 0.7 copy-done.1
  3.4 0.1 convert_reduce_fusion
  4.1 0.6 copy-done.2
  4.8 0.1 convolution_bitcast_fusion.3
  4.9 0.2 convolution_bitcast_fusion.4
  5.1 40.5 %all-reduce = (f32[64]{0:T(128)S(1)}, f32[64]{0:T(128)S(1)}) all-reduce(f32[64]{0:T(128)S(1)} %convolution_bitcast_fusion.4, f32[64]{0:T(128)S(1)} %convolution_bitcast_fusion.3), channel_id=1, replica_groups=mesh['gx'=4,'gy'=8] {'gx','gy'}, use_global_device_ids=true, to_apply=%region_2.3 | all-reduce | flops 128 | bytes 1024 | tf_op jit(solution)/shard_map/psum | solution.py:111
  45.6 0.1 broadcast_multiply_fusion.2
  47.8 0.3 select_select_fusion.1
  48.2 5.3 %collective-permute-start = (f32[5,8,128]{2,1,0:T(8,128)S(1)}, f32[5,8,128]{2,1,0:T(8,128)S(1)}, u32[]{:S(2)}, u32[]{:S(2)}) collective-permute-start(f32[5,8,128]{2,1,0:T(8,128)S(1)} %get-tuple-element.153), channel_id=1, source_target_pairs={{0,8},{8,16},{16,24},{1,9},{9,17},{17,25},{2,10},{10,18},{18,26},{... | collective-permute-start | bytes 61448 | tf_op jit(solution)/shard_map/ppermute | solution.py:44
  53.5 1.9 %collective-permute-start.1 = (f32[5,8,128]{2,1,0:T(8,128)S(1)}, f32[5,8,128]{2,1,0:T(8,128)S(1)}, u32[]{:S(2)}, u32[]{:S(2)}) collective-permute-start(f32[5,8,128]{2,1,0:T(8,128)S(1)} %get-tuple-element.154), channel_id=1, source_target_pairs={{8,0},{16,8},{24,16},{9,1},{17,9},{25,17},{10,2},{18,10},{26,18},{... | collective-permute-start | bytes 61448 | tf_op jit(solution)/shard_map/ppermute | solution.py:44
  55.5 3.1 %collective-permute-done.1 = f32[5,8,128]{2,1,0:T(8,128)S(1)} collective-permute-done((f32[5,8,128]{2,1,0:T(8,128)S(1)}, f32[5,8,128]{2,1,0:T(8,128)S(1)}, u32[]{:S(2)}, u32[]{:S(2)}) %collective-permute-start.1) | collective-permute-done | bytes 20512 | tf_op jit(solution)/shard_map/ppermute | solution.py:44
  58.7 0.3 collective-permute-start.2
  59.2 4.0 %collective-permute-start.3 = (f32[5,10,128]{2,0,1:T(8,128)S(1)}, f32[5,10,128]{2,0,1:T(8,128)S(1)}, u32[]{:S(2)}, u32[]{:S(2)}) collective-permute-start(f32[5,10,128]{2,0,1:T(8,128)S(1)} %stack.147), channel_id=1, source_target_pairs={{0,7},{1,0},{2,1},{3,2},{4,3},{5,4},{6,5},{7,6},{8,15},{9,8},{10,9... | collective-permute-start | bytes 76808 | tf_op jit(solution)/shard_map/ppermute | solution.py:50
  63.2 1.1 collective-permute-done.2
  65.7 0.3 constant_dynamic-update-slice_fusion.152
  66.8 0.1 fusion.168
  67.0 0.1 convolution_bitcast_fusion.1
  67.2 38.7 %psum.26 = f32[64]{0:T(128)S(1)} all-reduce(f32[64]{0:T(128)S(1)} %convolution_bitcast_fusion.1), channel_id=1, replica_groups=mesh['gx'=4,'gy'=8] {'gx','gy'}, use_global_device_ids=true, to_apply=%region_6.7 | all-reduce | flops 64 | bytes 512 | tf_op jit(solution)/shard_map/psum | solution.py:111
  105.9 0.1 broadcast_multiply_fusion.1
  106.3 0.1 constant_dynamic-update-slice_fusion.94
  107.7 0.3 select_select_fusion
  108.2 5.3 %collective-permute-start.4 = (f32[5,8,128]{2,1,0:T(8,128)S(1)}, f32[5,8,128]{2,1,0:T(8,128)S(1)}, u32[]{:S(2)}, u32[]{:S(2)}) collective-permute-start(f32[5,8,128]{2,1,0:T(8,128)S(1)} %get-tuple-element.125), channel_id=1, source_target_pairs={{0,8},{8,16},{16,24},{1,9},{9,17},{17,25},{2,10},{10,18},{18,26},{... | collective-permute-start | bytes 61448 | tf_op jit(solution)/shard_map/ppermute | solution.py:44
  113.4 1.9 %collective-permute-start.5 = (f32[5,8,128]{2,1,0:T(8,128)S(1)}, f32[5,8,128]{2,1,0:T(8,128)S(1)}, u32[]{:S(2)}, u32[]{:S(2)}) collective-permute-start(f32[5,8,128]{2,1,0:T(8,128)S(1)} %get-tuple-element.124), channel_id=1, source_target_pairs={{8,0},{16,8},{24,16},{9,1},{17,9},{25,17},{10,2},{18,10},{26,18},{... | collective-permute-start | bytes 61448 | tf_op jit(solution)/shard_map/ppermute | solution.py:44
  115.4 0.6 pad_maximum_fusion.164
  116.0 2.6 %collective-permute-done.5 = f32[5,8,128]{2,1,0:T(8,128)S(1)} collective-permute-done((f32[5,8,128]{2,1,0:T(8,128)S(1)}, f32[5,8,128]{2,1,0:T(8,128)S(1)}, u32[]{:S(2)}, u32[]{:S(2)}) %collective-permute-start.5) | collective-permute-done | bytes 20512 | tf_op jit(solution)/shard_map/ppermute | solution.py:44
  118.7 0.8 collective-permute-start.7
  119.5 0.7 collective-permute-start.6
  120.7 4.5 %collective-permute-done.6 = f32[5,10,128]{2,0,1:T(8,128)S(1)} collective-permute-done((f32[5,10,128]{2,0,1:T(8,128)S(1)}, f32[5,10,128]{2,0,1:T(8,128)S(1)}, u32[]{:S(2)}, u32[]{:S(2)}) %collective-permute-start.6) | collective-permute-done | bytes 25632 | tf_op jit(solution)/shard_map/ppermute | solution.py:50
  126.9 0.8 copy-done.3
  (263 shorter events, 8.4 us)
Async XLA Ops:
  0.6 2.0 %copy-start = (f32[19,8,8,128]{3,2,1,0:T(8,128)S(1)}, f32[19,8,8,128]{3,2,1,0:T(8,128)}, u32[]{:S(2)}) copy-start(f32[19,8,8,128]{3,2,1,0:T(8,128)} %param.3) | copy-start | bytes 1867780
  2.6 0.8 copy-start.1
  4.0 0.7 copy-start.2
  48.2 10.4 %collective-permute-start = (f32[5,8,128]{2,1,0:T(8,128)S(1)}, f32[5,8,128]{2,1,0:T(8,128)S(1)}, u32[]{:S(2)}, u32[]{:S(2)}) collective-permute-start(f32[5,8,128]{2,1,0:T(8,128)S(1)} %get-tuple-element.153), channel_id=1, source_target_pairs={{0,8},{8,16},{16,24},{1,9},{9,17},{17,25},{2,10},{10,18},{18,26},{... | collective-permute-start | bytes 61448 | tf_op jit(solution)/shard_map/ppermute | solution.py:44
  53.5 5.1 %collective-permute-start.1 = (f32[5,8,128]{2,1,0:T(8,128)S(1)}, f32[5,8,128]{2,1,0:T(8,128)S(1)}, u32[]{:S(2)}, u32[]{:S(2)}) collective-permute-start(f32[5,8,128]{2,1,0:T(8,128)S(1)} %get-tuple-element.154), channel_id=1, source_target_pairs={{8,0},{16,8},{24,16},{9,1},{17,9},{25,17},{10,2},{18,10},{26,18},{... | collective-permute-start | bytes 61448 | tf_op jit(solution)/shard_map/ppermute | solution.py:44
  58.7 5.6 %collective-permute-start.2 = (f32[5,10,128]{2,0,1:T(8,128)S(1)}, f32[5,10,128]{2,0,1:T(8,128)S(1)}, u32[]{:S(2)}, u32[]{:S(2)}) collective-permute-start(f32[5,10,128]{2,0,1:T(8,128)S(1)} %stack.145), channel_id=1, source_target_pairs={{0,1},{1,2},{2,3},{3,4},{4,5},{5,6},{6,7},{7,0},{8,9},{9,10},{10,1... | collective-permute-start | bytes 76808 | tf_op jit(solution)/shard_map/ppermute | solution.py:50
  59.2 5.2 %collective-permute-start.3 = (f32[5,10,128]{2,0,1:T(8,128)S(1)}, f32[5,10,128]{2,0,1:T(8,128)S(1)}, u32[]{:S(2)}, u32[]{:S(2)}) collective-permute-start(f32[5,10,128]{2,0,1:T(8,128)S(1)} %stack.147), channel_id=1, source_target_pairs={{0,7},{1,0},{2,1},{3,2},{4,3},{5,4},{6,5},{7,6},{8,15},{9,8},{10,9... | collective-permute-start | bytes 76808 | tf_op jit(solution)/shard_map/ppermute | solution.py:50
  108.2 7.8 %collective-permute-start.4 = (f32[5,8,128]{2,1,0:T(8,128)S(1)}, f32[5,8,128]{2,1,0:T(8,128)S(1)}, u32[]{:S(2)}, u32[]{:S(2)}) collective-permute-start(f32[5,8,128]{2,1,0:T(8,128)S(1)} %get-tuple-element.125), channel_id=1, source_target_pairs={{0,8},{8,16},{16,24},{1,9},{9,17},{17,25},{2,10},{10,18},{18,26},{... | collective-permute-start | bytes 61448 | tf_op jit(solution)/shard_map/ppermute | solution.py:44
  113.4 5.1 %collective-permute-start.5 = (f32[5,8,128]{2,1,0:T(8,128)S(1)}, f32[5,8,128]{2,1,0:T(8,128)S(1)}, u32[]{:S(2)}, u32[]{:S(2)}) collective-permute-start(f32[5,8,128]{2,1,0:T(8,128)S(1)} %get-tuple-element.124), channel_id=1, source_target_pairs={{8,0},{16,8},{24,16},{9,1},{17,9},{25,17},{10,2},{18,10},{26,18},{... | collective-permute-start | bytes 61448 | tf_op jit(solution)/shard_map/ppermute | solution.py:44
  118.7 6.9 %collective-permute-start.7 = (f32[5,10,128]{2,0,1:T(8,128)S(1)}, f32[5,10,128]{2,0,1:T(8,128)S(1)}, u32[]{:S(2)}, u32[]{:S(2)}) collective-permute-start(f32[5,10,128]{2,0,1:T(8,128)S(1)} %stack.347), channel_id=1, source_target_pairs={{0,7},{1,0},{2,1},{3,2},{4,3},{5,4},{6,5},{7,6},{8,15},{9,8},{10,9... | collective-permute-start | bytes 76808 | tf_op jit(solution)/shard_map/ppermute | solution.py:50
  119.5 5.6 %collective-permute-start.6 = (f32[5,10,128]{2,0,1:T(8,128)S(1)}, f32[5,10,128]{2,0,1:T(8,128)S(1)}, u32[]{:S(2)}, u32[]{:S(2)}) collective-permute-start(f32[5,10,128]{2,0,1:T(8,128)S(1)} %stack.172), channel_id=1, source_target_pairs={{0,1},{1,2},{2,3},{3,4},{4,5},{5,6},{6,7},{7,0},{8,9},{9,10},{10,1... | collective-permute-start | bytes 76808 | tf_op jit(solution)/shard_map/ppermute | solution.py:50
  126.9 0.8 copy-start.3
where the time goes:
time: 128 us
  blocking collectives  79.2 us (62%)
  starting transfers between devices  20.2 us (16%)
  waiting for transfers between devices  11.3 us (9%)
  other arithmetic  8.05 us (6%)
  local copies, waits for them, and re-layouts  6.31 us (5%)
  between operations  2.01 us (2%)
    psum x2, blocking collectives, outlet_mean(): totals, counts = lax.psum((local_sums, local_counts), ('gx', 'gy'))  79.2 us
    ppermute x4, starting transfers between devices, from_behind(): return lax.ppermute(block, axis, route)  14.4 us
    ppermute x4, starting transfers between devices, from_behind_2(): return lax.ppermute(value, axis, pairs)  5.84 us
    ppermute x4, waiting for transfers between devices, from_behind(): return lax.ppermute(block, axis, route)  5.67 us
    ppermute x4, waiting for transfers between devices, from_behind_2(): return lax.ppermute(value, axis, pairs)  5.62 us
    unnamed x80, other arithmetic  4.53 us
    unnamed x79, local copies, waits for them, and re-layouts  3.4 us
  transfers between devices with their start and end apart: 8, of which 4 were waited for; matrix products, arithmetic and copies ran while one was open for 1% of the time, Pallas kernels for 0%

commit v1 on v0

v1 whole, which is shorter than its diff:
```python
import functools

import jax
import jax.numpy as jnp
from jax import lax
from jax.experimental import pallas as pl
from jax.experimental.pallas import tpu as pltpu
from jax.sharding import PartitionSpec as P

REGIONS = 64
TILE = 4
VELOCITIES = (
    (0, 0, 0),
    (1, 0, 0),
    (-1, 0, 0),
    (0, 1, 0),
    (0, -1, 0),
    (0, 0, 1),
    (0, 0, -1),
    (1, 1, 0),
    (-1, -1, 0),
    (1, -1, 0),
    (-1, 1, 0),
    (1, 0, 1),
    (-1, 0, -1),
    (1, 0, -1),
    (-1, 0, 1),
    (0, 1, 1),
    (0, -1, -1),
    (0, 1, -1),
    (0, -1, 1),
)
NUMBER = {velocity: number for number, velocity in enumerate(VELOCITIES)}
WEIGHTS = (1.0 / 3.0,) + (1.0 / 18.0,) * 6 + (1.0 / 36.0,) * 12
OPPOSITE = (0, 2, 1, 4, 3, 6, 5, 8, 7, 10, 9, 12, 11, 14, 13, 16, 15, 18, 17)
RELAX_TIME = 0.8
INLET_SPEED = 0.05
RISING_X = (1, 7, 9, 11, 13)
FALLING_X = (2, 8, 10, 12, 14)
RISING_Y = (3, 7, 10, 15, 17)
FALLING_Y = (4, 8, 9, 16, 18)
SLOTS = RISING_X + FALLING_X + (0, 3, 4, 5, 6, 15, 16, 17, 18)
SLOT = {number: slot for slot, number in enumerate(SLOTS)}
MESH = pl.DeviceIdType.MESH


def inlet_value(number):
    comp_z = VELOCITIES[number][2]
    projected = comp_z * INLET_SPEED
    return WEIGHTS[number] * (
        1.0 + 3.0 * projected + 4.5 * projected * projected - 1.5 * INLET_SPEED * INLET_SPEED
    )


def signed_sum(terms):
    total = None
    for sign, value in terms:
        if total is None:
            total = value if sign > 0 else -value
        else:
            total = total + value if sign > 0 else total - value
    return total


def collide(current, kinds, outlet_density):
    density = functools.reduce(lambda a, b: a + b, current)
    inverse = 1.0 / density
    vel = [
        signed_sum([(v[d], current[n]) for n, v in enumerate(VELOCITIES) if v[d] != 0]) * inverse
        for d in range(3)
    ]
    base = 1.0 - 1.5 * (vel[0] * vel[0] + vel[1] * vel[1] + vel[2] * vel[2])
    wall = kinds == 1
    inlet = kinds == 2
    outlet = kinds == 3
    keep = jnp.where(outlet, 0.0, 1.0 - 1.0 / RELAX_TIME)
    scale = jnp.where(outlet, outlet_density, density * (1.0 / RELAX_TIME))
    scales = {w: scale * w for w in sorted(set(WEIGHTS))}
    post = [None] * 19
    for number in range(19):
        if number > OPPOSITE[number]:
            continue
        other = OPPOSITE[number]
        if number == 0:
            pairs = ((0, base),)
        else:
            projected = signed_sum([(c, vel[d]) for d, c in enumerate(VELOCITIES[number]) if c])
            even = base + 4.5 * projected * projected
            odd = 3.0 * projected
            pairs = ((number, even + odd), (other, even - odd))
        for n, unit in pairs:
            moved = keep * current[n] + scales[WEIGHTS[n]] * unit
            moved = jnp.where(inlet, inlet_value(n), moved)
            post[n] = jnp.where(wall, current[OPPOSITE[n]], moved)
    return density, post


def kernel(
    ngx,
    ngy,
    cx,
    cy,
    region_ref,
    pops_ref,
    kind_ref,
    out_ref,
    means_ref,
    post_a,
    post_b,
    density_ref,
    up_a,
    down_a,
    up_b,
    down_b,
    low_a,
    high_a,
    low_b,
    high_b,
    row_ref,
    table,
    spread,
    mult,
    mult_low,
    mult_high,
    send_sems,
    recv_sems,
    gather_sems,
):
    gx = lax.axis_index("gx")
    gy = lax.axis_index("gy")
    count = ngx * ngy
    me = gx * ngy + gy
    tx_n, ty_n = cx // TILE, cy // TILE
    nz = pops_ref.shape[3]
    lane = lax.broadcasted_iota(jnp.int32, (1, 128), 1)
    zlane = lax.broadcasted_iota(jnp.int32, (cy, nz), 1)
    yrow = lax.broadcasted_iota(jnp.int32, (cy, nz), 0)

    barrier = pltpu.get_barrier_semaphore()

    def greet(k, carry):
        peer = lax.rem(me + k, count)
        pl.semaphore_signal(
            barrier, inc=1, device_id={"gx": peer // ngy, "gy": peer % ngy}, device_id_type=MESH
        )
        return carry

    lax.fori_loop(1, count, greet, 0)

    def first(x, carry):
        current = [pops_ref[n, x] for n in range(19)]
        density, post = collide(current, kind_ref[x], 1.0)
        density_ref[x] = density
        for n in range(19):
            post_a[SLOT[n], x + 1] = post[n]
        for k in range(5):
            up_a[k, x] = post[RISING_Y[k]][cy - 1 :, :]
            down_a[k, x] = post[FALLING_Y[k]][:1, :]
        return carry

    lax.fori_loop(0, cx, first, 0)

    sums = {}

    def put(key, value):
        sums[key] = value if key not in sums else sums[key] + value

    for tx in range(tx_n):
        for i in range(TILE):
            x = tx * TILE + i
            for vx in (-1, 0, 1):
                dx = vx if (vx == 1 and i == TILE - 1) or (vx == -1 and i == 0) else 0
                for vy in (-1, 0, 1):
                    flat = jnp.where(
                        zlane == nz - 1, post_a[SLOT[NUMBER[(vx, vy, 0)]], x + 1], 0.0
                    )
                    if (vx, vy, 1) in NUMBER:
                        rising = post_a[SLOT[NUMBER[(vx, vy, 1)]], x + 1]
                        falling = post_a[SLOT[NUMBER[(vx, vy, -1)]], x + 1]
                        flat = jnp.where(zlane == nz - 2, rising, flat)
                        flat = jnp.where(zlane == 0, falling, flat)
                    put((tx, dx, vy), flat)
            put((tx, "rho"), jnp.where(zlane == nz - 1, density_ref[x], 0.0))
    stage = jnp.zeros((cy, 128), jnp.float32)
    lane8 = lax.broadcasted_iota(jnp.int32, (cy, 128), 1)
    row8 = lax.broadcasted_iota(jnp.int32, (cy, 128), 0)
    block = 16 * ty_n
    for tx in range(tx_n):
        for dx in (-1, 0, 1):
            for vy in (-1, 0, 1):
                value = sums[(tx, dx, vy)]
                fixed = jnp.sum(jnp.where(zlane == nz - 1, 0.0, value), axis=1, keepdims=True)
                scaled = jnp.sum(jnp.where(zlane == nz - 1, value, 0.0), axis=1, keepdims=True)
                at = tx * block + (dx + 1) * 4 + vy + 1
                stage = jnp.where(lane8 == at, fixed, stage)
                stage = jnp.where(lane8 == 64 + at, scaled, stage)
        rho = jnp.sum(sums[(tx, "rho")], axis=1, keepdims=True)
        stage = jnp.where(lane8 == tx * block + 13, rho, stage)
    slot8 = lane8 & 3
    message = jnp.zeros((1, 128), jnp.float32)
    for ty in range(ty_n):
        first_row, last_row = ty * TILE, ty * TILE + TILE - 1
        inside = (row8 >= first_row) & (row8 <= last_row)
        crossing = ((slot8 == 2) & (row8 == last_row)) | ((slot8 == 0) & (row8 == first_row))
        cross = jnp.sum(jnp.where(crossing, stage, 0.0), axis=0, keepdims=True)
        stay = jnp.where(inside & jnp.logical_not(crossing), stage, 0.0)
        stay = jnp.broadcast_to(jnp.sum(stay, axis=0, keepdims=True), (8, 128))
        stay = (stay + pltpu.roll(stay, 1, 1) + pltpu.roll(stay, 127, 1))[:1]
        both = jnp.where((lane & 3) == 1, stay, cross)
        if ty:
            both = pltpu.roll(jnp.broadcast_to(both, (8, 128)), 16 * ty, 1)[:1]
        message = message + both
    for tx in range(tx_n):
        for ty in range(ty_n):
            region = region_ref[tx * TILE, ty * TILE].astype(jnp.float32)
            message = jnp.where(lane == 64 + tx * block + ty * 16 + 13, region, message)
    row_ref[...] = message
    table[me] = message

    pl.semaphore_wait(barrier, count - 1)

    def spread_row(k, carry):
        peer = lax.rem(me + k, count)
        pltpu.make_async_remote_copy(
            src_ref=row_ref,
            dst_ref=table.at[me],
            send_sem=gather_sems.at[0],
            recv_sem=gather_sems.at[1],
            device_id={"gx": peer // ngy, "gy": peer % ngy},
            device_id_type=MESH,
        ).start()
        return carry

    lax.fori_loop(1, count, spread_row, 0)

    def exchange(step, post, up, down, low, high):
        def send(k, source, target, ox, oy):
            copy = pltpu.make_async_remote_copy(
                src_ref=source,
                dst_ref=target,
                send_sem=send_sems.at[step, k],
                recv_sem=recv_sems.at[step, k],
                device_id={"gx": lax.rem(gx + ox + ngx, ngx), "gy": lax.rem(gy + oy + ngy, ngy)},
                device_id_type=MESH,
            )
            copy.start()
            return copy

        return [
            send(0, up.at[RISING_Y.index(7), cx - 1], low.at[RISING_Y.index(7), 0], 1, 1),
            send(1, up.at[RISING_Y.index(10), 0], low.at[RISING_Y.index(10), cx + 1], -1, 1),
            send(2, down.at[FALLING_Y.index(9), cx - 1], high.at[FALLING_Y.index(9), 0], 1, -1),
            send(3, down.at[FALLING_Y.index(8), 0], high.at[FALLING_Y.index(8), cx + 1], -1, -1),
            send(4, up, low.at[:, pl.ds(1, cx)], 0, 1),
            send(5, down, high.at[:, pl.ds(1, cx)], 0, -1),
            send(6, post.at[pl.ds(0, 5), cx], post.at[pl.ds(0, 5), 0], 1, 0),
            send(7, post.at[pl.ds(5, 5), 1], post.at[pl.ds(5, 5), cx + 1], -1, 0),
        ]

    def rims(post, low, high):
        @pl.when(gx == 0)
        def _():
            post[0:5, 0] = jnp.zeros((5, cy, nz), jnp.float32)
            low[RISING_Y.index(7), 0] = jnp.zeros((1, nz), jnp.float32)
            high[FALLING_Y.index(9), 0] = jnp.zeros((1, nz), jnp.float32)

        @pl.when(gx == ngx - 1)
        def _():
            post[5:10, cx + 1] = jnp.zeros((5, cy, nz), jnp.float32)
            low[RISING_Y.index(10), cx + 1] = jnp.zeros((1, nz), jnp.float32)
            high[FALLING_Y.index(8), cx + 1] = jnp.zeros((1, nz), jnp.float32)

    copies = exchange(0, post_a, up_a, down_a, low_a, high_a)

    whole = pltpu.make_async_copy(
        table.at[pl.ds(0, count - 1)], table.at[pl.ds(0, count - 1)], gather_sems.at[1]
    )
    whole.wait()
    pltpu.make_async_copy(
        table.at[pl.ds(0, count - 1)], table.at[pl.ds(0, count - 1)], gather_sems.at[0]
    ).wait()

    tiles = tx_n * ty_n
    lanes = lax.broadcasted_iota(jnp.int32, (ngy, 128), 1)
    lanes_f = lanes.astype(jnp.float32)
    rows = [table[pl.ds(X * ngy, ngy), 0, :] for X in range(ngx)]
    onehot = {}
    total = jnp.zeros((ngy, 128), jnp.float32)
    cells = jnp.zeros((ngy, 128), jnp.float32)
    for X in range(ngx):
        for q in range(tiles):
            at = q * 16 + 13
            onehot[X, q] = rows[X][:, 64 + at : 65 + at] == lanes_f
            total = total + jnp.where(onehot[X, q], rows[X][:, at : at + 1], 0.0)
            cells = cells + jnp.where(onehot[X, q], 1.0 * TILE * TILE, 0.0)
    cells = jnp.sum(cells, axis=0, keepdims=True)
    cells = jnp.where(cells > 0.0, cells, 1.0)
    mean_1 = jnp.sum(total, axis=0, keepdims=True) / cells
    means_ref[0:1, :] = mean_1[:, :REGIONS]

    tile_x, tile_y = (lanes >> 4) // ty_n, (lanes >> 4) % ty_n
    step_x, step_y = ((lanes >> 2) & 3) - 1, (lanes & 3) - 1
    real = (lanes < 16 * tiles) & (step_x < 2) & (step_y < 2)
    to_x, to_y = tile_x + step_x, tile_y + step_y
    off_x = jnp.where(to_x < 0, -1, jnp.where(to_x >= tx_n, 1, 0))
    off_y = jnp.where(to_y < 0, -1, jnp.where(to_y >= ty_n, 1, 0))
    goal = (to_x - off_x * tx_n) * ty_n + (to_y - off_y * ty_n)
    shifted = []
    for X in range(ngx):
        by_tile = jnp.zeros((ngy, 128), jnp.float32)
        for q in range(tiles):
            m = jnp.sum(jnp.where(onehot[X, q], mean_1, 0.0), axis=1, keepdims=True)
            by_tile = jnp.where((lanes >> 4) == q, m, by_tile)
        spread[X] = by_tile
        value = jnp.where(real, rows[X] + by_tile * pltpu.roll(rows[X], 64, 1), 0.0)
        moved = jnp.where(off_y == 0, value, 0.0)
        moved = moved + pltpu.roll(jnp.where(off_y == 1, value, 0.0), 1, 0)
        moved = moved + pltpu.roll(jnp.where(off_y == -1, value, 0.0), ngy - 1, 0)
        shifted.append(moved)
    total = jnp.zeros((ngy, 128), jnp.float32)
    for X in range(ngx):
        landed = jnp.where(off_x == 0, shifted[X], 0.0)
        if X > 0:
            landed = landed + jnp.where(off_x == 1, shifted[X - 1], 0.0)
        if X < ngx - 1:
            landed = landed + jnp.where(off_x == -1, shifted[X + 1], 0.0)
        for q in range(tiles):
            s = jnp.sum(jnp.where(goal == q, landed, 0.0), axis=1, keepdims=True)
            total = total + jnp.where(onehot[X, q], s, 0.0)
    mean_2 = jnp.sum(total, axis=0, keepdims=True) / cells
    means_ref[1:2, :] = mean_2[:, :REGIONS]

    around = {}
    for ox in (-1, 0, 1):
        for oy in (-1, 0, 1):
            sx = jnp.clip(gx + ox, 0, ngx - 1)
            sy = lax.rem(gy + oy + ngy, ngy)
            around[ox, oy] = spread[sx, pl.ds(sy, 1), :]

    def tile_mean(tx, ty):
        ox = -1 if tx < 0 else 1 if tx >= tx_n else 0
        oy = -1 if ty < 0 else 1 if ty >= ty_n else 0
        at = ((tx - ox * tx_n) * ty_n + ty - oy * ty_n) * 16
        return around[ox, oy][:, at : at + 1]

    def columns(values):
        result = values[0]
        for ty in range(1, ty_n):
            result = jnp.where(yrow >= ty * TILE, values[ty], result)
        return result

    zrow = lax.broadcasted_iota(jnp.int32, (1, nz), 1)
    for k in range(tx_n + 2):
        mult[k] = jnp.where(
            zlane == nz - 1, columns([tile_mean(k - 1, ty) for ty in range(ty_n)]), 1.0
        )
        mult_low[k] = jnp.where(zrow == nz - 1, tile_mean(k - 1, -1), 1.0)
        mult_high[k] = jnp.where(zrow == nz - 1, tile_mean(k - 1, ty_n), 1.0)
    outlet_2 = []
    for tx in range(tx_n):
        values = []
        for ty in range(ty_n):
            mine = lane == region_ref[tx * TILE, ty * TILE]
            values.append(jnp.sum(jnp.where(mine, mean_2, 0.0), axis=1, keepdims=True))
        outlet_2.append(columns(values) + jnp.zeros((cy, nz), jnp.float32))

    for copy in copies:
        copy.wait()
    rims(post_a, low_a, high_a)

    def streamed(n, x, post, low, high, scaled):
        vx, vy, vz = VELOCITIES[n]
        source = x + 1 - vx
        block_of = (source + TILE - 1) // TILE
        value = post[SLOT[n], source]
        if scaled:
            value = value * mult[block_of]
        if vy == 1:
            edge = low[RISING_Y.index(n), source]
            edge = edge * mult_low[block_of] if scaled else edge
            value = jnp.where(yrow == 0, edge, pltpu.roll(value, 1, 0))
        elif vy == -1:
            edge = high[FALLING_Y.index(n), source]
            edge = edge * mult_high[block_of] if scaled else edge
            value = jnp.where(yrow == cy - 1, edge, pltpu.roll(value, cy - 1, 0))
        if vz:
            value = pltpu.roll(value, vz % nz, 1)
        return value

    for tx in range(tx_n):

        def second(x, carry):
            current = [streamed(n, x, post_a, low_a, high_a, True) for n in range(19)]
            _, post = collide(current, kind_ref[x], outlet_2[tx])
            for n in range(19):
                post_b[SLOT[n], x + 1] = post[n]
            for k in range(5):
                up_b[k, x] = post[RISING_Y[k]][cy - 1 :, :]
                down_b[k, x] = post[FALLING_Y[k]][:1, :]
            return carry

        lax.fori_loop(tx * TILE, tx * TILE + TILE, second, 0)

    copies = exchange(1, post_b, up_b, down_b, low_b, high_b)
    for copy in copies:
        copy.wait()
    rims(post_b, low_b, high_b)

    def last(x, carry):
        for n in range(19):
            out_ref[n, x] = streamed(n, x, post_b, low_b, high_b, False)
        return carry

    lax.fori_loop(0, cx, last, 0)


def solution(mesh):
    ngx, ngy = mesh.shape["gx"], mesh.shape["gy"]

    def body(populations, cell_kind, outlet_region):
        _, cx, cy, nz = populations.shape
        f32 = jnp.float32
        return pl.pallas_call(
            functools.partial(kernel, ngx, ngy, cx, cy),
            out_shape=(
                jax.ShapeDtypeStruct(populations.shape, f32),
                jax.ShapeDtypeStruct((2, REGIONS), f32),
            ),
            in_specs=[
                pl.BlockSpec(memory_space=pltpu.SMEM),
                pl.BlockSpec(memory_space=pltpu.VMEM),
                pl.BlockSpec(memory_space=pltpu.VMEM),
            ],
            out_specs=(
                pl.BlockSpec(memory_space=pltpu.VMEM),
                pl.BlockSpec(memory_space=pltpu.VMEM),
            ),
            scratch_shapes=[
                pltpu.VMEM((19, cx + 2, cy, nz), f32),
                pltpu.VMEM((19, cx + 2, cy, nz), f32),
                pltpu.VMEM((cx, cy, nz), f32),
                pltpu.VMEM((5, cx, 1, nz), f32),
                pltpu.VMEM((5, cx, 1, nz), f32),
                pltpu.VMEM((5, cx, 1, nz), f32),
                pltpu.VMEM((5, cx, 1, nz), f32),
                pltpu.VMEM((5, cx + 2, 1, nz), f32),
                pltpu.VMEM((5, cx + 2, 1, nz), f32),
                pltpu.VMEM((5, cx + 2, 1, nz), f32),
                pltpu.VMEM((5, cx + 2, 1, nz), f32),
                pltpu.VMEM((1, 128), f32),
                pltpu.VMEM((ngx * ngy, 1, 128), f32),
                pltpu.VMEM((ngx, ngy, 128), f32),
                pltpu.VMEM((cx // TILE + 2, cy, nz), f32),
                pltpu.VMEM((cx // TILE + 2, 1, nz), f32),
                pltpu.VMEM((cx // TILE + 2, 1, nz), f32),
                pltpu.SemaphoreType.DMA((2, 8)),
                pltpu.SemaphoreType.DMA((2, 8)),
                pltpu.SemaphoreType.DMA((2,)),
            ],
            compiler_params=pltpu.CompilerParams(collective_id=0, has_side_effects=True),
        )(outlet_region, populations, cell_kind)

    in_specs = (P(None, "gx", "gy", None), P("gx", "gy", None), P("gx", "gy"))
    out_specs = (P(None, "gx", "gy", None), P())
    return jax.shard_map(body, mesh=mesh, in_specs=in_specs, out_specs=out_specs, check_vma=False)
```

time: 128 us -> 23.8 us (0.19)
  blocking collectives: 79.2 us -> 0 us
  Pallas kernels: 0 us -> 20.2 us
  starting transfers between devices: 20.2 us -> 0 us
  waiting for transfers between devices: 11.3 us -> 0 us
  other arithmetic: 8.05 us -> 0 us
  local copies, waits for them, and re-layouts: 6.31 us -> 2.52 us
  between operations: 2.01 us -> 0.65 us
    psum x2 -> x0, blocking collectives: 79.2 us -> none  [outlet_mean(): totals, counts = lax.psum((local_sums, local_counts), ('gx', 'gy'))]
    ppermute x8 -> x0, starting transfers between devices: 20.2 us -> none  [the longest x4 14.4 us: from_behind(): return lax.ppermute(block, axis, route)]
    pallas_call x0 -> x1, Pallas kernels: none -> 20.2 us  [body(): pl.pallas_call(functools.partial(kernel, ngx, ngy, cx, cy), out_shape=(ja...]
    ppermute x8 -> x0, waiting for transfers between devices: 11.3 us -> none  [the longest x4 5.67 us: from_behind(): return lax.ppermute(block, axis, route)]
    unnamed x80 -> x0, other arithmetic: 4.53 us -> none
    slice x34 -> x0, local copies, waits for them, and re-layouts: 1.56 us -> none  [the longest x30 1.55 us: stream(): moved.append(jnp.roll(plane, comp_z, axis=2))]
    another operation x24 -> x0, other arithmetic: 1.53 us -> none  [the longest x1 0.57 us: body(): return (current, jnp.stack(means))]
    reduce_sum x3 -> x0, other arithmetic: 1.33 us -> none  [the longest x1 1.12 us: outlet_mean(): density = jnp.sum(current, axis=0)]
  transfers between devices with their start and end apart: 8 -> 0, of which waited for: 4 -> 0; matrix products, arithmetic and copies ran while one was open for 1% -> 0% of each run, Pallas kernels for 0% -> 0%
where the time goes in v1:
time: 23.8 us; the launch traced here: 23.3 us
  Pallas kernels  20.2 us (85%)
  local copies, waits for them, and re-layouts  2.52 us (11%)
  between operations  0.65 us (3%)
    pallas_call x1, Pallas kernels, body(): pl.pallas_call(functools.partial(kernel, ngx, ngy, cx, cy), out_shape=(ja...  20.2 us
    unnamed x4, local copies, waits for them, and re-layouts  2.52 us

profile of v1, /device:TPU:1, one launch (start us, length us, event | category | flops | bytes accessed | tf_op | source)
XLA Modules:
  0.0 23.3 jit_solution(2052337631106080877)
XLA Ops:
  0.6 20.2 %shard_map.50 = (f32[19,8,8,128]{3,2,1,0:T(8,128)}, f32[2,64]{1,0:T(2,128)}) custom-call(s32[8,8]{1,0:T(8,128)} %region_ref.1, f32[19,8,8,128]{3,2,1,0:T(8,128)} %pops_ref.1, s32[8,8,128]{2,1,0:T(8,128)} %kind_ref.1), custom_call_target="tpu_custom_call" | custom-call | tf_op jit(solution)/shard_map/pallas_call | solution.py:423
  20.8 0.0 copy-start
  20.8 2.0 %copy.7 = f32[19,8,8,128]{3,2,1,0:T(8,128)} copy(f32[19,8,8,128]{3,2,1,0:T(8,128)} %get-tuple-element.4) | data formatting | bytes 1245184
  22.8 0.0 copy-done
  22.8 0.6 %copy.8 = f32[2,64]{1,0:T(2,128)} copy(f32[2,64]{1,0:T(2,128)S(1)} %copy-done) | data formatting | bytes 1024
Async XLA Ops:
  20.8 2.0 %copy-start = (f32[2,64]{1,0:T(2,128)S(1)}, f32[2,64]{1,0:T(2,128)}, u32[]{:S(2)}) copy-start(f32[2,64]{1,0:T(2,128)} %get-tuple-element.5) | copy-start | bytes 1540

commit v2 on v1

--- a/solution.py
+++ b/solution.py
@@ -95,18 +95,56 @@
     return density, post
 
 
+def streamed(n, x, post, low, high, scales=None):
+    vx, vy, vz = VELOCITIES[n]
+    source = x + 1 - vx
+    cy, nz = post.shape[2:]
+    yrow = lax.broadcasted_iota(jnp.int32, (cy, nz), 0)
+    value = post[SLOT[n], source]
+    if scales:
+        scale, scale_low, scale_high = [ref[(source + TILE - 1) // TILE] for ref in scales]
+        value = value * scale
+    if vy == 1:
+        edge = low[RISING_Y.index(n), source]
+        edge = edge * scale_low if scales else edge
+        value = jnp.where(yrow == 0, edge, pltpu.roll(value, 1, 0))
+    elif vy == -1:
+        edge = high[FALLING_Y.index(n), source]
+        edge = edge * scale_high if scales else edge
+        value = jnp.where(yrow == cy - 1, edge, pltpu.roll(value, cy - 1, 0))
+    if vz:
+        value = pltpu.roll(value, vz % nz, 1)
+    return value
+
+
+def finish(post, low, high, means, out_hbm, means_out, out_ref, sems):
+    means_out[...] = means[...]
+    copies = []
+    for n in range(19):
+        for x in range(out_ref.shape[1]):
+            out_ref[n, x] = streamed(n, x, post, low, high)
+        copies.append(pltpu.make_async_copy(out_ref.at[n], out_hbm.at[n], sems.at[n]))
+        copies[-1].start()
+    for copy in copies:
+        copy.wait()
+
+
 def kernel(
     ngx,
     ngy,
     cx,
     cy,
     region_ref,
+    pops_hbm,
+    kind_hbm,
+    post_b,
+    low_b,
+    high_b,
+    means_ref,
     pops_ref,
     kind_ref,
-    out_ref,
-    means_ref,
+    load_sems,
     post_a,
-    post_b,
     density_ref,
     up_a,
     down_a,
@@ -114,8 +152,6 @@
     down_b,
     low_a,
     high_a,
-    low_b,
-    high_b,
     row_ref,
     table,
     spread,
@@ -136,16 +172,30 @@
     zlane = lax.broadcasted_iota(jnp.int32, (cy, nz), 1)
     yrow = lax.broadcasted_iota(jnp.int32, (cy, nz), 0)
 
+    loads = [
+        pltpu.make_async_copy(pops_hbm, pops_ref, load_sems.at[0]),
+        pltpu.make_async_copy(kind_hbm, kind_ref, load_sems.at[1]),
+    ]
+    for load in loads:
+        load.start()
     barrier = pltpu.get_barrier_semaphore()
 
-    def greet(k, carry):
-        peer = lax.rem(me + k, count)
-        pl.semaphore_signal(
-            barrier, inc=1, device_id={"gx": peer // ngy, "gy": peer % ngy}, device_id_type=MESH
-        )
-        return carry
-
-    lax.fori_loop(1, count, greet, 0)
+    def wrapped(value, size):
+        return jnp.where(value >= size, value - size, value)
+
+    def every_peer(visit):
+        for ox in range(ngx):
+            px = wrapped(gx + ox, ngx)
+
+            def one(oy, carry):
+                visit({"gx": px, "gy": wrapped(gy + oy, ngy)})
+                return carry
+
+            lax.fori_loop(0 if ox else 1, ngy, one, 0, unroll=ngy <= 8)
+
+    every_peer(
+        lambda peer: pl.semaphore_signal(barrier, inc=1, device_id=peer, device_id_type=MESH)
+    )
 
     def first(x, carry):
         current = [pops_ref[n, x] for n in range(19)]
@@ -158,6 +208,8 @@
             down_a[k, x] = post[FALLING_Y[k]][:1, :]
         return carry
 
+    for load in loads:
+        load.wait()
     lax.fori_loop(0, cx, first, 0)
 
     sums = {}
@@ -219,19 +271,16 @@
 
     pl.semaphore_wait(barrier, count - 1)
 
-    def spread_row(k, carry):
-        peer = lax.rem(me + k, count)
-        pltpu.make_async_remote_copy(
+    every_peer(
+        lambda peer: pltpu.make_async_remote_copy(
             src_ref=row_ref,
             dst_ref=table.at[me],
             send_sem=gather_sems.at[0],
             recv_sem=gather_sems.at[1],
-            device_id={"gx": peer // ngy, "gy": peer % ngy},
+            device_id=peer,
             device_id_type=MESH,
         ).start()
-        return carry
-
-    lax.fori_loop(1, count, spread_row, 0)
+    )
 
     def exchange(step, post, up, down, low, high):
         def send(k, source, target, ox, oy):
@@ -368,29 +417,10 @@
         copy.wait()
     rims(post_a, low_a, high_a)
 
-    def streamed(n, x, post, low, high, scaled):
-        vx, vy, vz = VELOCITIES[n]
-        source = x + 1 - vx
-        block_of = (source + TILE - 1) // TILE
-        value = post[SLOT[n], source]
-        if scaled:
-            value = value * mult[block_of]
-        if vy == 1:
-            edge = low[RISING_Y.index(n), source]
-            edge = edge * mult_low[block_of] if scaled else edge
-            value = jnp.where(yrow == 0, edge, pltpu.roll(value, 1, 0))
-        elif vy == -1:
-            edge = high[FALLING_Y.index(n), source]
-            edge = edge * mult_high[block_of] if scaled else edge
-            value = jnp.where(yrow == cy - 1, edge, pltpu.roll(value, cy - 1, 0))
-        if vz:
-            value = pltpu.roll(value, vz % nz, 1)
-        return value
-
     for tx in range(tx_n):
 
         def second(x, carry):
-            current = [streamed(n, x, post_a, low_a, high_a, True) for n in range(19)]
+            current = [streamed(n, x, post_a, low_a, high_a, (mult, mult_low, mult_high)) for n in range(19)]
             _, post = collide(current, kind_ref[x], outlet_2[tx])
             for n in range(19):
                 post_b[SLOT[n], x + 1] = post[n]
@@ -406,13 +436,6 @@
         copy.wait()
     rims(post_b, low_b, high_b)
 
-    def last(x, carry):
-        for n in range(19):
-            out_ref[n, x] = streamed(n, x, post_b, low_b, high_b, False)
-        return carry
-
-    lax.fori_loop(0, cx, last, 0)
-
 
 def solution(mesh):
     ngx, ngy = mesh.shape["gx"], mesh.shape["gy"]
@@ -420,31 +443,28 @@
     def body(populations, cell_kind, outlet_region):
         _, cx, cy, nz = populations.shape
         f32 = jnp.float32
-        return pl.pallas_call(
+        vmem = pl.BlockSpec(memory_space=pltpu.VMEM)
+        hbm = pl.BlockSpec(memory_space=pltpu.HBM)
+        middle = pl.pallas_call(
             functools.partial(kernel, ngx, ngy, cx, cy),
             out_shape=(
-                jax.ShapeDtypeStruct(populations.shape, f32),
-                jax.ShapeDtypeStruct((2, REGIONS), f32),
+                pltpu.VMEM((19, cx + 2, cy, nz), f32),
+                pltpu.VMEM((5, cx + 2, 1, nz), f32),
+                pltpu.VMEM((5, cx + 2, 1, nz), f32),
+                pltpu.VMEM((2, REGIONS), f32),
             ),
-            in_specs=[
-                pl.BlockSpec(memory_space=pltpu.SMEM),
-                pl.BlockSpec(memory_space=pltpu.VMEM),
-                pl.BlockSpec(memory_space=pltpu.VMEM),
-            ],
-            out_specs=(
-                pl.BlockSpec(memory_space=pltpu.VMEM),
-                pl.BlockSpec(memory_space=pltpu.VMEM),
-            ),
+            in_specs=[pl.BlockSpec(memory_space=pltpu.SMEM), hbm, hbm],
+            out_specs=(vmem, vmem, vmem, vmem),
             scratch_shapes=[
-                pltpu.VMEM((19, cx + 2, cy, nz), f32),
+                pltpu.VMEM(populations.shape, f32),
+                pltpu.VMEM(cell_kind.shape, jnp.int32),
+                pltpu.SemaphoreType.DMA((2,)),
                 pltpu.VMEM((19, cx + 2, cy, nz), f32),
                 pltpu.VMEM((cx, cy, nz), f32),
                 pltpu.VMEM((5, cx, 1, nz), f32),
                 pltpu.VMEM((5, cx, 1, nz), f32),
                 pltpu.VMEM((5, cx, 1, nz), f32),
                 pltpu.VMEM((5, cx, 1, nz), f32),
-                pltpu.VMEM((5, cx + 2, 1, nz), f32),
-                pltpu.VMEM((5, cx + 2, 1, nz), f32),
                 pltpu.VMEM((5, cx + 2, 1, nz), f32),
                 pltpu.VMEM((5, cx + 2, 1, nz), f32),
                 pltpu.VMEM((1, 128), f32),
@@ -457,8 +477,24 @@
                 pltpu.SemaphoreType.DMA((2, 8)),
                 pltpu.SemaphoreType.DMA((2,)),
             ],
-            compiler_params=pltpu.CompilerParams(collective_id=0, has_side_effects=True),
+            compiler_params=pltpu.CompilerParams(
+                collective_id=0, has_side_effects=True, vmem_limit_bytes=48 * 2**20
+            ),
         )(outlet_region, populations, cell_kind)
+        return pl.pallas_call(
+            finish,
+            out_shape=(
+                jax.ShapeDtypeStruct(populations.shape, f32),
+                jax.ShapeDtypeStruct((2, REGIONS), f32),
+            ),
+            in_specs=[vmem, vmem, vmem, vmem],
+            out_specs=(hbm, vmem),
+            scratch_shapes=[
+                pltpu.VMEM(populations.shape, f32),
+                pltpu.SemaphoreType.DMA((19,)),
+            ],
+            compiler_params=pltpu.CompilerParams(vmem_limit_bytes=16 * 2**20),
+        )(*middle)
 
     in_specs = (P(None, "gx", "gy", None), P("gx", "gy", None), P("gx", "gy"))
     out_specs = (P(None, "gx", "gy", None), P())

time: 23.8 us -> 23.3 us (0.979)
  Pallas kernels: 20.2 us -> 19.8 us
    pallas_call x1 -> x2, Pallas kernels: 20.2 us -> 19.8 us  [the longest x1 18.3 us: body(): pl.pallas_call(functools.partial(kernel, ngx, ngy, cx, cy), out_shape=(pl...]
    unnamed x4 -> x6, local copies, waits for them, and re-layouts: 2.52 us -> 2.51 us
where the time goes in v2:
time: 23.3 us; the launch traced here: 23 us
  Pallas kernels  19.8 us (85%)
  local copies, waits for them, and re-layouts  2.51 us (11%)
  between operations  0.65 us (3%)
    pallas_call x1, Pallas kernels, body(): pl.pallas_call(functools.partial(kernel, ngx, ngy, cx, cy), out_shape=(pl...  18.3 us
    unnamed x6, local copies, waits for them, and re-layouts  2.51 us
    pallas_call x1, Pallas kernels, body(): pl.pallas_call(finish, out_shape=(jax.ShapeDtypeStruct(populations.shape,...  1.56 us

profile of v2, /device:TPU:1, one launch (start us, length us, event | category | flops | bytes accessed | tf_op | source)
XLA Modules:
  0.0 23.0 jit_solution(12891888216809464537)
XLA Ops:
  0.6 0.0 copy-start
  0.6 1.1 %copy-done = f32[19,8,8,128]{3,2,1,0:T(8,128)S(1)} copy-done((f32[19,8,8,128]{3,2,1,0:T(8,128)S(1)}, f32[19,8,8,128]{3,2,1,0:T(8,128)}, u32[]{:S(2)}) %copy-start) | copy-done | bytes 622616
  1.7 0.0 copy-start.1
  1.7 0.8 %copy-done.1 = s32[8,8,128]{2,1,0:T(8,128)S(1)} copy-done((s32[8,8,128]{2,1,0:T(8,128)S(1)}, s32[8,8,128]{2,1,0:T(8,128)}, u32[]{:S(2)}) %copy-start.1) | copy-done | bytes 32792
  2.5 0.0 copy-start.2
  2.5 0.7 %copy-done.2 = s32[8,8]{1,0:T(8,128)S(1)} copy-done((s32[8,8]{1,0:T(8,128)S(1)}, s32[8,8]{1,0:T(8,128)}, u32[]{:S(2)}) %copy-start.2) | copy-done | bytes 280
  3.2 18.3 %shard_map.50 = (f32[19,10,8,128]{3,2,1,0:T(8,128)S(1)}, f32[5,10,1,128]{3,2,1,0:T(1,128)S(1)}, f32[5,10,1,128]{3,2,1,0:T(1,128)S(1)}, f32[2,64]{1,0:T(2,128)S(1)}) custom-call(s32[8,8]{1,0:T(8,128)S(1)} %copy-done.2, f32[19,8,8,128]{3,2,1,0:T(8,128)S(1)} %copy-done, s32[8,8,128]{2,1,0:T(8,128)S(1)} %copy-done.1), custom_call_target="tpu_custom_call" | custom-call | tf_op jit(solution)/shard_map/pallas_call | solution.py:448
  21.4 1.6 %shard_map.51 = (f32[19,8,8,128]{3,2,1,0:T(8,128)}, f32[2,64]{1,0:T(2,128)}) custom-call(f32[19,10,8,128]{3,2,1,0:T(8,128)S(1)} %get-tuple-element.6.post, f32[5,10,1,128]{3,2,1,0:T(1,128)S(1)} %get-tuple-element.7.low, f32[5,10,1,128]{3,2,1,0:T(1,128)S(1)} %get-tuple-element.8.high, f32[2,64]{1,0:T(2,128)S(1)} %get-tuple-element.9.means), custom_call_target="tpu_custom_call" | custom-call | tf_op jit(solution)/shard_map/pallas_call | solution.py:484
Async XLA Ops:
  0.6 1.1 %copy-start = (f32[19,8,8,128]{3,2,1,0:T(8,128)S(1)}, f32[19,8,8,128]{3,2,1,0:T(8,128)}, u32[]{:S(2)}) copy-start(f32[19,8,8,128]{3,2,1,0:T(8,128)} %pops_hbm.1) | copy-start | bytes 1867780
  1.7 0.8 %copy-start.1 = (s32[8,8,128]{2,1,0:T(8,128)S(1)}, s32[8,8,128]{2,1,0:T(8,128)}, u32[]{:S(2)}) copy-start(s32[8,8,128]{2,1,0:T(8,128)} %kind_hbm.1) | copy-start | bytes 98308
  2.5 0.7 %copy-start.2 = (s32[8,8]{1,0:T(8,128)S(1)}, s32[8,8]{1,0:T(8,128)}, u32[]{:S(2)}) copy-start(s32[8,8]{1,0:T(8,128)} %region_ref.1) | copy-start | bytes 772

commit v3 on v2

--- a/solution.py
+++ b/solution.py
@@ -134,13 +134,14 @@
     ngy,
     cx,
     cy,
-    region_ref,
+    region_hbm,
     pops_hbm,
     kind_hbm,
     post_b,
     low_b,
     high_b,
     means_ref,
+    region_ref,
     pops_ref,
     kind_ref,
     load_sems,
@@ -173,6 +174,7 @@
     yrow = lax.broadcasted_iota(jnp.int32, (cy, nz), 0)
 
     loads = [
+        pltpu.make_async_copy(region_hbm, region_ref, load_sems.at[2]),
         pltpu.make_async_copy(pops_hbm, pops_ref, load_sems.at[0]),
         pltpu.make_async_copy(kind_hbm, kind_ref, load_sems.at[1]),
     ]
@@ -443,6 +445,7 @@
     def body(populations, cell_kind, outlet_region):
         _, cx, cy, nz = populations.shape
         f32 = jnp.float32
+        arrays = (outlet_region, populations, cell_kind)
         vmem = pl.BlockSpec(memory_space=pltpu.VMEM)
         hbm = pl.BlockSpec(memory_space=pltpu.HBM)
         middle = pl.pallas_call(
@@ -453,12 +456,13 @@
                 pltpu.VMEM((5, cx + 2, 1, nz), f32),
                 pltpu.VMEM((2, REGIONS), f32),
             ),
-            in_specs=[pl.BlockSpec(memory_space=pltpu.SMEM), hbm, hbm],
+            in_specs=[hbm, hbm, hbm],
             out_specs=(vmem, vmem, vmem, vmem),
             scratch_shapes=[
+                pltpu.SMEM(outlet_region.shape, jnp.int32),
                 pltpu.VMEM(populations.shape, f32),
                 pltpu.VMEM(cell_kind.shape, jnp.int32),
-                pltpu.SemaphoreType.DMA((2,)),
+                pltpu.SemaphoreType.DMA((3,)),
                 pltpu.VMEM((19, cx + 2, cy, nz), f32),
                 pltpu.VMEM((cx, cy, nz), f32),
                 pltpu.VMEM((5, cx, 1, nz), f32),
@@ -480,7 +484,7 @@
             compiler_params=pltpu.CompilerParams(
                 collective_id=0, has_side_effects=True, vmem_limit_bytes=48 * 2**20
             ),
-        )(outlet_region, populations, cell_kind)
+        )(*[pltpu.with_memory_space_constraint(a, pltpu.HBM) for a in arrays])
         return pl.pallas_call(
             finish,
             out_shape=(

time: 23.3 us -> 19.9 us (0.85)
  local copies, waits for them, and re-layouts: 2.51 us -> 0 us
  Pallas kernels: 19.8 us -> 19.1 us
    unnamed x6 -> x0, local copies, waits for them, and re-layouts: 2.51 us -> none
    pallas_call x1, Pallas kernels: 18.3 us -> 17.5 us  [body(): pl.pallas_call(functools.partial(kernel, ngx, ngy, cx, cy), out_shape=(pl...]
where the time goes in v3:
time: 19.9 us; the launch traced here: 19.7 us
  Pallas kernels  19.1 us (96%)
  between operations  0.64 us (3%)
    pallas_call x1, Pallas kernels, body(): pl.pallas_call(functools.partial(kernel, ngx, ngy, cx, cy), out_shape=(pl...  17.5 us
    pallas_call x1, Pallas kernels, body(): pl.pallas_call(finish, out_shape=(jax.ShapeDtypeStruct(populations.shape,...  1.56 us

profile of v3, /device:TPU:1, one launch (start us, length us, event | category | flops | bytes accessed | tf_op | source)
XLA Modules:
  0.0 19.7 jit_solution(10074248500498477337)
XLA Ops:
  0.6 17.5 %shard_map.50 = (f32[19,10,8,128]{3,2,1,0:T(8,128)S(1)}, f32[5,10,1,128]{3,2,1,0:T(1,128)S(1)}, f32[5,10,1,128]{3,2,1,0:T(1,128)S(1)}, f32[2,64]{1,0:T(2,128)S(1)}) custom-call(s32[8,8]{1,0:T(8,128)} %region_hbm.1, f32[19,8,8,128]{3,2,1,0:T(8,128)} %pops_hbm.1, s32[8,8,128]{2,1,0:T(8,128)} %kind_hbm.1), custom_call_target="tpu_custom_call" | custom-call | tf_op jit(solution)/shard_map/pallas_call | solution.py:451
  18.1 1.6 %shard_map.51 = (f32[19,8,8,128]{3,2,1,0:T(8,128)}, f32[2,64]{1,0:T(2,128)}) custom-call(f32[19,10,8,128]{3,2,1,0:T(8,128)S(1)} %get-tuple-element.6.post, f32[5,10,1,128]{3,2,1,0:T(1,128)S(1)} %get-tuple-element.7.low, f32[5,10,1,128]{3,2,1,0:T(1,128)S(1)} %get-tuple-element.8.high, f32[2,64]{1,0:T(2,128)S(1)} %get-tuple-element.9.means), custom_call_target="tpu_custom_call" | custom-call | tf_op jit(solution)/shard_map/pallas_call | solution.py:488

commit v4 on v3

--- a/solution.py
+++ b/solution.py
@@ -117,12 +117,12 @@
     return value
 
 
-def finish(post, low, high, means, out_hbm, means_out, out_ref, sems):
+def finish(post, low, high, means, mult, mult_low, mult_high, out_hbm, means_out, out_ref, sems):
     means_out[...] = means[...]
     copies = []
     for n in range(19):
         for x in range(out_ref.shape[1]):
-            out_ref[n, x] = streamed(n, x, post, low, high)
+            out_ref[n, x] = streamed(n, x, post, low, high, (mult, mult_low, mult_high))
         copies.append(pltpu.make_async_copy(out_ref.at[n], out_hbm.at[n], sems.at[n]))
         copies[-1].start()
     for copy in copies:
@@ -141,6 +141,9 @@
     low_b,
     high_b,
     means_ref,
+    mult_b,
+    mult_low_b,
+    mult_high_b,
     region_ref,
     pops_ref,
     kind_ref,
@@ -186,14 +189,19 @@
         return jnp.where(value >= size, value - size, value)
 
     def every_peer(visit):
-        for ox in range(ngx):
-            px = wrapped(gx + ox, ngx)
-
-            def one(oy, carry):
-                visit({"gx": px, "gy": wrapped(gy + oy, ngy)})
+        for turn in range(ngy):
+            away = ngy - (turn + 1) // 2 if turn % 2 else turn // 2
+            py = wrapped(ngy - 1 - gy + away, ngy)
+
+            def one(ox, carry):
+                visit({"gx": wrapped(gx + ox, ngx), "gy": py})
                 return carry
 
-            lax.fori_loop(0 if ox else 1, ngy, one, 0, unroll=ngy <= 8)
+            @pl.when(py != gy)
+            def _():
+                visit({"gx": gx, "gy": py})
+
+            lax.fori_loop(1, ngx, one, 0, unroll=ngx <= 4)
 
     every_peer(
         lambda peer: pl.semaphore_signal(barrier, inc=1, device_id=peer, device_id_type=MESH)
@@ -349,6 +357,63 @@
     mean_1 = jnp.sum(total, axis=0, keepdims=True) / cells
     means_ref[0:1, :] = mean_1[:, :REGIONS]
 
+    def by_region(mean, X):
+        result = jnp.zeros((ngy, 128), jnp.float32)
+        for q in range(tiles):
+            m = jnp.sum(jnp.where(onehot[X, q], mean, 0.0), axis=1, keepdims=True)
+            result = jnp.where((lanes >> 4) == q, m, result)
+        return result
+
+    by_tile = [by_region(mean_1, X) for X in range(ngx)]
+    for X in range(ngx):
+        spread[0, X] = by_tile[X]
+
+    zrow = lax.broadcasted_iota(jnp.int32, (1, nz), 1)
+
+    def scale_outlets(step, mult, mult_low, mult_high):
+        around = {}
+        for ox in (-1, 0, 1):
+            for oy in (-1, 0, 1):
+                sx = jnp.clip(gx + ox, 0, ngx - 1)
+                sy = lax.rem(gy + oy + ngy, ngy)
+                around[ox, oy] = spread[step, sx, pl.ds(sy, 1), :]
+
+        def tile_mean(tx, ty):
+            ox = -1 if tx < 0 else 1 if tx >= tx_n else 0
+            oy = -1 if ty < 0 else 1 if ty >= ty_n else 0
+            at = ((tx - ox * tx_n) * ty_n + ty - oy * ty_n) * 16
+            return around[ox, oy][:, at : at + 1]
+
+        for k in range(tx_n + 2):
+            column = tile_mean(k - 1, 0)
+            for ty in range(1, ty_n):
+                column = jnp.where(yrow >= ty * TILE, tile_mean(k - 1, ty), column)
+            mult[k] = jnp.where(zlane == nz - 1, column, 1.0)
+            mult_low[k] = jnp.where(zrow == nz - 1, tile_mean(k - 1, -1), 1.0)
+            mult_high[k] = jnp.where(zrow == nz - 1, tile_mean(k - 1, ty_n), 1.0)
+
+    scale_outlets(0, mult, mult_low, mult_high)
+
+    for copy in copies:
+        copy.wait()
+    rims(post_a, low_a, high_a)
+
+    def second(x, carry):
+        current = [
+            streamed(n, x, post_a, low_a, high_a, (mult, mult_low, mult_high)) for n in range(19)
+        ]
+        _, post = collide(current, kind_ref[x], 1.0)
+        for n in range(19):
+            post_b[SLOT[n], x + 1] = post[n]
+        for k in range(5):
+            up_b[k, x] = post[RISING_Y[k]][cy - 1 :, :]
+            down_b[k, x] = post[FALLING_Y[k]][:1, :]
+        return carry
+
+    lax.fori_loop(0, cx, second, 0)
+
+    copies = exchange(1, post_b, up_b, down_b, low_b, high_b)
+
     tile_x, tile_y = (lanes >> 4) // ty_n, (lanes >> 4) % ty_n
     step_x, step_y = ((lanes >> 2) & 3) - 1, (lanes & 3) - 1
     real = (lanes < 16 * tiles) & (step_x < 2) & (step_y < 2)
@@ -358,12 +423,7 @@
     goal = (to_x - off_x * tx_n) * ty_n + (to_y - off_y * ty_n)
     shifted = []
     for X in range(ngx):
-        by_tile = jnp.zeros((ngy, 128), jnp.float32)
-        for q in range(tiles):
-            m = jnp.sum(jnp.where(onehot[X, q], mean_1, 0.0), axis=1, keepdims=True)
-            by_tile = jnp.where((lanes >> 4) == q, m, by_tile)
-        spread[X] = by_tile
-        value = jnp.where(real, rows[X] + by_tile * pltpu.roll(rows[X], 64, 1), 0.0)
+        value = jnp.where(real, rows[X] + by_tile[X] * pltpu.roll(rows[X], 64, 1), 0.0)
         moved = jnp.where(off_y == 0, value, 0.0)
         moved = moved + pltpu.roll(jnp.where(off_y == 1, value, 0.0), 1, 0)
         moved = moved + pltpu.roll(jnp.where(off_y == -1, value, 0.0), ngy - 1, 0)
@@ -381,59 +441,10 @@
     mean_2 = jnp.sum(total, axis=0, keepdims=True) / cells
     means_ref[1:2, :] = mean_2[:, :REGIONS]
 
-    around = {}
-    for ox in (-1, 0, 1):
-        for oy in (-1, 0, 1):
-            sx = jnp.clip(gx + ox, 0, ngx - 1)
-            sy = lax.rem(gy + oy + ngy, ngy)
-            around[ox, oy] = spread[sx, pl.ds(sy, 1), :]
-
-    def tile_mean(tx, ty):
-        ox = -1 if tx < 0 else 1 if tx >= tx_n else 0
-        oy = -1 if ty < 0 else 1 if ty >= ty_n else 0
-        at = ((tx - ox * tx_n) * ty_n + ty - oy * ty_n) * 16
-        return around[ox, oy][:, at : at + 1]
-
-    def columns(values):
-        result = values[0]
-        for ty in range(1, ty_n):
-            result = jnp.where(yrow >= ty * TILE, values[ty], result)
-        return result
-
-    zrow = lax.broadcasted_iota(jnp.int32, (1, nz), 1)
-    for k in range(tx_n + 2):
-        mult[k] = jnp.where(
-            zlane == nz - 1, columns([tile_mean(k - 1, ty) for ty in range(ty_n)]), 1.0
-        )
-        mult_low[k] = jnp.where(zrow == nz - 1, tile_mean(k - 1, -1), 1.0)
-        mult_high[k] = jnp.where(zrow == nz - 1, tile_mean(k - 1, ty_n), 1.0)
-    outlet_2 = []
-    for tx in range(tx_n):
-        values = []
-        for ty in range(ty_n):
-            mine = lane == region_ref[tx * TILE, ty * TILE]
-            values.append(jnp.sum(jnp.where(mine, mean_2, 0.0), axis=1, keepdims=True))
-        outlet_2.append(columns(values) + jnp.zeros((cy, nz), jnp.float32))
-
-    for copy in copies:
-        copy.wait()
-    rims(post_a, low_a, high_a)
-
-    for tx in range(tx_n):
-
-        def second(x, carry):
-            current = [streamed(n, x, post_a, low_a, high_a, (mult, mult_low, mult_high)) for n in range(19)]
-            _, post = collide(current, kind_ref[x], outlet_2[tx])
-            for n in range(19):
-                post_b[SLOT[n], x + 1] = post[n]
-            for k in range(5):
-                up_b[k, x] = post[RISING_Y[k]][cy - 1 :, :]
-                down_b[k, x] = post[FALLING_Y[k]][:1, :]
-            return carry
-
-        lax.fori_loop(tx * TILE, tx * TILE + TILE, second, 0)
-
-    copies = exchange(1, post_b, up_b, down_b, low_b, high_b)
+    for X in range(ngx):
+        spread[1, X] = by_region(mean_2, X)
+    scale_outlets(1, mult_b, mult_low_b, mult_high_b)
+
     for copy in copies:
         copy.wait()
     rims(post_b, low_b, high_b)
@@ -455,9 +466,12 @@
                 pltpu.VMEM((5, cx + 2, 1, nz), f32),
                 pltpu.VMEM((5, cx + 2, 1, nz), f32),
                 pltpu.VMEM((2, REGIONS), f32),
+                pltpu.VMEM((cx // TILE + 2, cy, nz), f32),
+                pltpu.VMEM((cx // TILE + 2, 1, nz), f32),
+                pltpu.VMEM((cx // TILE + 2, 1, nz), f32),
             ),
             in_specs=[hbm, hbm, hbm],
-            out_specs=(vmem, vmem, vmem, vmem),
+            out_specs=(vmem,) * 7,
             scratch_shapes=[
                 pltpu.SMEM(outlet_region.shape, jnp.int32),
                 pltpu.VMEM(populations.shape, f32),
@@ -473,7 +487,7 @@
                 pltpu.VMEM((5, cx + 2, 1, nz), f32),
                 pltpu.VMEM((1, 128), f32),
                 pltpu.VMEM((ngx * ngy, 1, 128), f32),
-                pltpu.VMEM((ngx, ngy, 128), f32),
+                pltpu.VMEM((2, ngx, ngy, 128), f32),
                 pltpu.VMEM((cx // TILE + 2, cy, nz), f32),
                 pltpu.VMEM((cx // TILE + 2, 1, nz), f32),
                 pltpu.VMEM((cx // TILE + 2, 1, nz), f32),
@@ -491,7 +505,7 @@
                 jax.ShapeDtypeStruct(populations.shape, f32),
                 jax.ShapeDtypeStruct((2, REGIONS), f32),
             ),
-            in_specs=[vmem, vmem, vmem, vmem],
+            in_specs=[vmem] * 7,
             out_specs=(hbm, vmem),
             scratch_shapes=[
                 pltpu.VMEM(populations.shape, f32),

time: 19.9 us -> 19.6 us (0.985)
  Pallas kernels: 19.1 us -> 18.8 us
    pallas_call x1, Pallas kernels: 17.5 us -> 17.2 us  [body(): pl.pallas_call(functools.partial(kernel, ngx, ngy, cx, cy), out_shape=(pl...]
where the time goes in v4:
time: 19.6 us; the launch traced here: 19.4 us
  Pallas kernels  18.8 us (96%)
  between operations  0.64 us (3%)
    pallas_call x1, Pallas kernels, body(): pl.pallas_call(functools.partial(kernel, ngx, ngy, cx, cy), out_shape=(pl...  17.2 us
    pallas_call x1, Pallas kernels, body(): pl.pallas_call(finish, out_shape=(jax.ShapeDtypeStruct(populations.shape,...  1.57 us

profile of v4, /device:TPU:1, one launch (start us, length us, event | category | flops | bytes accessed | tf_op | source)
XLA Modules:
  0.0 19.4 jit_solution(11540120732669675954)
XLA Ops:
  0.6 17.2 %shard_map.50 = (f32[19,10,8,128]{3,2,1,0:T(8,128)S(1)}, f32[5,10,1,128]{3,2,1,0:T(1,128)S(1)}, f32[5,10,1,128]{3,2,1,0:T(1,128)S(1)}, f32[2,64]{1,0:T(2,128)S(1...) custom-call(s32[8,8]{1,0:T(8,128)} %region_hbm.1, f32[19,8,8,128]{3,2,1,0:T(8,128)} %pops_hbm.1, ...), custom_call_target="tpu_custom_call" | custom-call | tf_op jit(solution)/shard_map/pallas_call | solution.py:462
  17.8 1.6 %shard_map.51 = (f32[19,8,8,128]{3,2,1,0:T(8,128)}, f32[2,64]{1,0:T(2,128)}) custom-call(f32[19,10,8,128]{3,2,1,0:T(8,128)S(1)} %get-tuple-element.9.post, f32[5,10,1,128]{3,2,1,0:T(1,128)S(1)} %get-tuple-element.10.low, f32[5,10,1,128]{3,2,1,0:T(1,128)S(1)} %get-tuple-element.11.high, f32[2,64]{1,0:T(2,128)S(1)} %get-tuple-element.12.means, ...), custom_call_target="tpu_custom_call" | custom-call | tf_op jit(solution)/shard_map/pallas_call | solution.py:502

commit v5 on v4

--- a/solution.py
+++ b/solution.py
@@ -220,7 +220,7 @@
 
     for load in loads:
         load.wait()
-    lax.fori_loop(0, cx, first, 0)
+    lax.fori_loop(0, cx, first, 0, unroll=2)
 
     sums = {}
 
@@ -410,7 +410,7 @@
             down_b[k, x] = post[FALLING_Y[k]][:1, :]
         return carry
 
-    lax.fori_loop(0, cx, second, 0)
+    lax.fori_loop(0, cx, second, 0, unroll=cx)
 
     copies = exchange(1, post_b, up_b, down_b, low_b, high_b)
 

time: 19.6 us -> 19.1 us (0.974)
  Pallas kernels: 18.8 us -> 18.3 us
    pallas_call x1, Pallas kernels: 17.2 us -> 16.7 us  [body(): pl.pallas_call(functools.partial(kernel, ngx, ngy, cx, cy), out_shape=(pl...]
where the time goes in v5:
time: 19.1 us; the launch traced here: 18.9 us
  Pallas kernels  18.3 us (96%)
  between operations  0.64 us (3%)
    pallas_call x1, Pallas kernels, body(): pl.pallas_call(functools.partial(kernel, ngx, ngy, cx, cy), out_shape=(pl...  16.7 us
    pallas_call x1, Pallas kernels, body(): pl.pallas_call(finish, out_shape=(jax.ShapeDtypeStruct(populations.shape,...  1.57 us

profile of v5, /device:TPU:1, one launch (start us, length us, event | category | flops | bytes accessed | tf_op | source)
XLA Modules:
  0.0 18.9 jit_solution(9658859610056993488)
XLA Ops:
  0.6 16.7 %shard_map.50 = (f32[19,10,8,128]{3,2,1,0:T(8,128)S(1)}, f32[5,10,1,128]{3,2,1,0:T(1,128)S(1)}, f32[5,10,1,128]{3,2,1,0:T(1,128)S(1)}, f32[2,64]{1,0:T(2,128)S(1...) custom-call(s32[8,8]{1,0:T(8,128)} %region_hbm.1, f32[19,8,8,128]{3,2,1,0:T(8,128)} %pops_hbm.1, ...), custom_call_target="tpu_custom_call" | custom-call | tf_op jit(solution)/shard_map/pallas_call | solution.py:462
  17.3 1.6 %shard_map.51 = (f32[19,8,8,128]{3,2,1,0:T(8,128)}, f32[2,64]{1,0:T(2,128)}) custom-call(f32[19,10,8,128]{3,2,1,0:T(8,128)S(1)} %get-tuple-element.9.post, f32[5,10,1,128]{3,2,1,0:T(1,128)S(1)} %get-tuple-element.10.low, f32[5,10,1,128]{3,2,1,0:T(1,128)S(1)} %get-tuple-element.11.high, f32[2,64]{1,0:T(2,128)S(1)} %get-tuple-element.12.means, ...), custom_call_target="tpu_custom_call" | custom-call | tf_op jit(solution)/shard_map/pallas_call | solution.py:502
